TPU v7x, 256 devices: a whole 4x4x8 slice. The times are simulated.
256 devices in a mesh: ctx: 32 (over x, z_lo, core), tp: 8 (over z_hi, y).
Axes of the slice: x: 4, y: 4, z: 8 (z_hi: 2, z_lo: 4; z = z_hi * 4 + z_lo), core: 2. Of those that a mesh axis runs over, the one named last changes fastest.
Arguments:
- token_ids: int32 [24576], P('ctx'), may hold values from 0 to 511
- embed_table: bfloat16 [512, 4096], replicated, may hold values from -6 to 6
- norm_gain: float32 [4096], replicated, may hold values from 0.25 to 1.75
- w_in: bfloat16 [4096, 3, 2048], P(None, None, 'tp'), may hold values from -0.09375 to 0.09375
- short_taps: float32 [3, 3, 2048], P(None, None, 'tp'), may hold values from -3 to 3
- long_filter: bfloat16 [2048, 24576], P('tp', 'ctx'), may hold values from -0.0390625 to 0.0390625
- skip_gain: float32 [2048], P('tp'), may hold values from 0.5 to 2
- w_out: bfloat16 [2048, 4096], P(None, 'tp'), may hold values from -0.125 to 0.125
Outputs:
- mixed: bfloat16 [24576, 4096], P('ctx', 'tp')
All inputs are finite; a program needn't handle non-finite values.
Results may differ from a plain program's by a relative error of at most 0.0095.
Values may be sent and summed in bfloat16 or wider, within the bound.
A program may use at most 128 MiB of HBM per device.

v0:
```python
import math
import jax
import jax.numpy as jnp
from jax import lax
from jax.sharding import Mesh
from jax.sharding import PartitionSpec as P

CTX = ("ctx_0", "ctx_1", "ctx_2")
norm_eps = 1e-06


def shifted(block, axis, distance):
    devices = range(lax.axis_size(axis))
    route = [(i - distance, i) for i in devices if i - distance in devices]
    return lax.ppermute(block, axis, route)


def sent_together(arrays, axis, split_dim, concat_dim, along):
    ends, at = ([], 0)
    for a in arrays[:-1]:
        at += a.shape[along]
        ends.append(at)
    both = jnp.concatenate(arrays, axis=along)
    return tuple(
        jnp.split(
            lax.all_to_all(both, axis, split_axis=split_dim, concat_axis=concat_dim, tiled=True),
            ends,
            axis=along,
        )
    )


def in_blocks(x, dim, peers):
    dims = x.shape
    pieces = x.reshape(*dims[:dim], peers, dims[dim] // peers, *dims[dim + 1 :])
    return jnp.moveaxis(pieces, dim, 0)


def in_order(pieces, dim):
    dims = list(pieces.shape[1:])
    dims[dim] *= pieces.shape[0]
    return jnp.moveaxis(pieces, 0, dim).reshape(dims)


def turned_blocks(pieces, axes, sequence):
    inside = pieces.shape[1:]
    out = pieces.reshape(*(lax.axis_size(a) for a in axes), *inside)
    for k in sequence:
        out = lax.all_to_all(out, axes[k], k, k, tiled=True)
    return out.reshape(-1, *inside)


def core_and_chips(x, groups, sequence, split_dim, concat_dim):
    peers = lax.axis_size(groups[0]) * lax.axis_size(groups[1])
    pieces = in_blocks(x, split_dim, peers)
    return in_order(turned_blocks(pieces, groups, sequence), concat_dim)


def angle_table(outer, inner, period):
    product = (
        jnp.arange(outer, dtype=jnp.int32)[:, None]
        * jnp.arange(inner, dtype=jnp.int32)[None, :]
        % period
    )
    phase = product.astype(jnp.float32) * (2.0 * math.pi / period)
    return (jnp.cos(phase), jnp.sin(phase))


def contract(form, left, right):
    return jnp.einsum(form, left, right, preferred_element_type=jnp.float32)


def forward_transform(signal, tables):
    cos_rows, sin_rows, cos_twist, sin_twist, cos_cols, sin_cols = tables
    first_real = contract("kn,cnm->ckm", cos_rows, signal)
    first_imag = -contract("kn,cnm->ckm", sin_rows, signal)
    turned_real = first_real * cos_twist + first_imag * sin_twist
    turned_imag = first_imag * cos_twist - first_real * sin_twist
    spec_real = contract("ckm,mj->ckj", turned_real, cos_cols) + contract(
        "ckm,mj->ckj", turned_imag, sin_cols
    )
    spec_imag = contract("ckm,mj->ckj", turned_imag, cos_cols) - contract(
        "ckm,mj->ckj", turned_real, sin_cols
    )
    return (spec_real, spec_imag)


def inverse_transform(spec_real, spec_imag, tables, period):
    cos_rows, sin_rows, cos_twist, sin_twist, cos_cols, sin_cols = tables
    back_real = contract("ckj,mj->ckm", spec_real, cos_cols) - contract(
        "ckj,mj->ckm", spec_imag, sin_cols
    )
    back_imag = contract("ckj,mj->ckm", spec_imag, cos_cols) + contract(
        "ckj,mj->ckm", spec_real, sin_cols
    )
    untwist_real = back_real * cos_twist - back_imag * sin_twist
    untwist_imag = back_imag * cos_twist + back_real * sin_twist
    signal = contract("kn,ckm->cnm", cos_rows, untwist_real) - contract(
        "kn,ckm->cnm", sin_rows, untwist_imag
    )
    return signal / period


def causal_conv(signal, kernel):
    channels = signal.shape[0]
    length = signal.shape[1]
    col_count = min(256, length)
    row_count = 2 * length // col_count
    half_rows = length // col_count
    cos_rows, sin_rows = angle_table(row_count, half_rows, row_count)
    cos_twist, sin_twist = angle_table(row_count, col_count, row_count * col_count)
    cos_cols, sin_cols = angle_table(col_count, col_count, col_count)
    tables = (cos_rows, sin_rows, cos_twist, sin_twist, cos_cols, sin_cols)
    signal_real, signal_imag = forward_transform(
        signal.astype(jnp.float32).reshape(channels, half_rows, col_count), tables
    )
    kernel_real, kernel_imag = forward_transform(
        kernel.astype(jnp.float32).reshape(channels, half_rows, col_count), tables
    )
    joint_real = signal_real * kernel_real - signal_imag * kernel_imag
    joint_imag = signal_real * kernel_imag + signal_imag * kernel_real
    result = inverse_transform(joint_real, joint_imag, tables, row_count * col_count)
    return result.reshape(channels, length)


def local(token_ids, embed_table, norm_gain, w_in, short_taps, long_filter, skip_gain, w_out):
    vocab = embed_table.shape[0]
    one_hot = (token_ids[:, None] == jnp.arange(vocab, dtype=jnp.int32)[None, :]).astype(
        jnp.bfloat16
    )
    embedded = jnp.dot(one_hot, embed_table, preferred_element_type=jnp.float32)
    scale = lax.rsqrt(jnp.mean(embedded * embedded, axis=1, keepdims=True) + norm_eps)
    normed = (embedded * scale * norm_gain).astype(jnp.bfloat16)
    width = w_in.shape[0]
    chan_part = w_in.shape[2]
    flat_proj = jnp.dot(
        normed, w_in.reshape(width, 3 * chan_part), preferred_element_type=jnp.float32
    ).astype(jnp.bfloat16)
    projected = jnp.transpose(flat_proj.reshape(-1, 3, chan_part), (1, 2, 0))
    positions = projected.shape[2]
    edge = projected[:, :, positions - 2 :]
    prior = shifted(edge, CTX, 1)
    extended = jnp.concatenate([prior, projected], axis=2).astype(jnp.float32)
    shortened = (
        short_taps[0][:, :, None] * extended[:, :, 2:]
        + short_taps[1][:, :, None] * extended[:, :, 1 : positions + 1]
        + short_taps[2][:, :, None] * extended[:, :, 0:positions]
    ).astype(jnp.bfloat16)
    query_side = shortened[0]
    key_side = shortened[1]
    value_side = shortened[2]
    local_channels = shortened.shape[1]
    groups = lax.axis_size(CTX)
    owned = local_channels // groups

    def spread(array):
        return array.reshape(groups, owned, array.shape[-1])

    first_channel = lax.axis_index(CTX) * owned
    own_skip = lax.dynamic_slice_in_dim(skip_gain, first_channel, owned)[:, None]
    product_local = (key_side.astype(jnp.float32) * value_side.astype(jnp.float32)).astype(
        jnp.bfloat16
    )
    arrived = sent_together((spread(product_local), spread(long_filter)), CTX, 0, 2, 1)
    product = arrived[0].reshape(owned, -1)
    filter_full = arrived[1].reshape(owned, -1)
    convolved = causal_conv(product, filter_full)
    outgoing = (convolved + own_skip * product.astype(jnp.float32)).astype(jnp.bfloat16)
    returned = core_and_chips(
        outgoing.reshape(1, owned, -1), (("ctx_0", "ctx_1"), "ctx_2"), (1, 0), 2, 0
    )
    returned = returned.reshape(local_channels, positions)
    gated = (query_side.astype(jnp.float32) * returned.astype(jnp.float32)).astype(jnp.bfloat16)
    width_part = w_out.shape[1]
    projected_out = jnp.dot(
        lax.all_gather(gated, "tp", axis=0, tiled=True).T, w_out, preferred_element_type=jnp.float32
    )
    residual = lax.dynamic_slice_in_dim(embedded, lax.axis_index("tp") * width_part, width_part, 1)
    return (residual + projected_out).astype(jnp.bfloat16)


def solution(mesh):
    finer = Mesh(mesh.devices.reshape(4, 4, 2, mesh.shape["tp"]), ("ctx_0", "ctx_1", "ctx_2", "tp"))
    in_specs = (
        P(CTX),
        P(),
        P(),
        P(None, None, "tp"),
        P(None, None, "tp"),
        P("tp", CTX),
        P("tp"),
        P(None, "tp"),
    )
    out_specs = P(CTX, "tp")
    return jax.shard_map(local, mesh=finer, in_specs=in_specs, out_specs=out_specs, check_vma=False)
```

profile of v0, /device:TPU:1, one launch (start us, length us, event | category | flops | bytes accessed | tf_op | source)
XLA Modules:
  0.0 231.1 jit_solution(8118276754307388498)
XLA Ops:
  6.5 0.0 copy-start
  6.5 8.8 %multiply_reduce_fusion = (f32[768]{0:T(1024)S(1)}, f32[768,4096]{1,0:T(8,128)}) fusion(bf16[512,4096]{1,0:T(8,128)(2,1)} %param.9, s32[768]{0:T(1024)} %param.8), kind=kOutput, calls=%fused_computation.1 | convolution fusion | flops 3227909376 | bytes 16783360 | tf_op jit(solution)/shard_map/dot_general | solution.py:131
  15.4 0.0 copy-start.4
  15.4 8.7 %copy.32 = bf16[4096,3,256]{0,2,1:T(8,128)(2,1)} copy(bf16[4096,3,256]{2,0,1:T(8,128)(2,1)} %param.11) | data formatting | bytes 12582912 | tf_op args[3]
  24.0 0.0 copy-done.4
  24.0 0.0 copy-start.3
  24.0 11.1 %fusion.19 = bf16[768,768]{0,1:T(8,128)(2,1)S(1)} fusion(bf16[4096,768]{0,1:T(8,128)(2,1)} %bitcast.149, f32[768,4096]{1,0:T(8,128)} %get-tuple-element.13, f32[4096]{0:T(1024)S(1)} %copy-done.4, f32[768]{0:T(1024)S(1)} %add_rsqrt_fusion), kind=kOutput, calls=%fused_computation.36 | convolution fusion | flops 4841865216 | bytes 20073472 | tf_op jit(solution)/shard_map/dot_general | solution.py:136
  35.1 0.1 slice.40
  35.2 4.9 %collective-permute-start = (bf16[3,256,2]{2,1,0:T(8,128)(2,1)S(1)}, bf16[3,256,2]{2,1,0:T(8,128)(2,1)S(1)}, u32[]{:S(2)}, u32[]{:S(2)}) collective-permute-start(bf16[3,256,2]{2,1,0:T(8,128)(2,1)S(1)} %slice.40), channel_id=1, source_target_pairs={{0,8},{8,16},{16,24},{24,32},{32,40},{40,48},{48,56},{56,64},{64,7... | collective-permute-start | bytes 9224 | tf_op jit(solution)/shard_map/ppermute | solution.py:15
  40.2 0.0 copy-done.3
  40.2 2.6 %collective-permute-done = bf16[3,256,2]{2,1,0:T(8,128)(2,1)S(1)} collective-permute-done((bf16[3,256,2]{2,1,0:T(8,128)(2,1)S(1)}, bf16[3,256,2]{2,1,0:T(8,128)(2,1)S(1)}, u32[]{:S(2)}, u32[]{:S(2)}) %collective-permute-start) | collective-permute-done | bytes 3104 | tf_op jit(solution)/shard_map/ppermute | solution.py:15
  42.7 0.6 maximum_convert_fusion
  43.3 0.0 copy-start.2
  43.4 2.0 fusion.4
  45.4 0.0 copy-start.1
  45.4 1.1 copy-done.1
  46.4 0.1 fusion.37
  46.5 0.0 copy-done.2
  46.6 0.0 copy-start.5
  46.6 0.9 pad_maximum_fusion
  47.5 9.5 %all-to-all-start = ((bf16[32,16,768]{2,1,0:T(8,128)(2,1)}), bf16[32,16,768]{2,1,0:T(8,128)(2,1)S(1)}, u32[]{:S(2)}, u32[]{:S(2)}) async-start(bf16[32,16,768]{2,1,0:T(8,128)(2,1)} %pad_maximum_fusion), calls=%async_computation | async-start | bytes 1572864 | tf_op jit(solution)/shard_map/all_to_all | solution.py:26
  57.0 0.2 all-gather.2.cloned.1.call-start
  57.2 0.0 copy-done.5
  57.2 0.1 dynamic_slice.7
  57.3 0.8 fusion.84
  58.1 21.2 %all-to-all-done = bf16[32,16,768]{2,1,0:T(8,128)(2,1)S(1)} async-done(((bf16[32,16,768]{2,1,0:T(8,128)(2,1)}), bf16[32,16,768]{2,1,0:T(8,128)(2,1)S(1)}, u32[]{:S(2)}, u32[]{:S(2)}) %all-to-all-start) | async-done | bytes 786464 | tf_op jit(solution)/shard_map/all_to_all | solution.py:26
  79.3 0.1 copy.49
  79.3 0.1 fusion.204
  79.4 0.8 convolution_negate_fusion
  80.2 0.8 fusion.39
  80.9 0.8 convolution_negate_fusion.1
  81.7 0.8 fusion.42
  82.5 1.4 fusion.54
  83.9 1.4 fusion.58
  85.3 1.4 fusion.52
  86.7 1.4 fusion.48
  88.1 1.5 convolution_subtract_fusion.1
  89.5 1.4 convolution_add_fusion.2
  91.0 1.7 convolution_add_fusion.1
  92.7 1.8 multiply_add_fusion
  94.4 1.3 fusion.69
  95.8 1.3 fusion.71
  97.1 1.3 convolution_add_fusion
  98.4 1.3 convolution_subtract_fusion
  99.7 0.8 fusion.10
  100.5 1.7 fusion.26
  102.1 2.2 reshape.119
  104.4 1.6 fusion.31
  106.0 3.8 %all_to_all.28 = bf16[16,2,1,8,768]{4,3,0,2,1:T(8,128)(2,1)S(1)} all-to-all(bf16[16,2,1,8,768]{4,3,0,2,1:T(8,128)(2,1)S(1)} %copy.39), channel_id=1, replica_groups=mesh['ctx_0'=4,'ctx_1'=4,'ctx_2'=2,'tp'=8] {'ctx_2'}, dimensions={1} | all-to-all | bytes 786432 | tf_op jit(solution)/shard_map/all_to_all | solution.py:49
  109.8 16.1 %all_to_all.29 = bf16[16,2,1,8,768]{4,3,1,2,0:T(8,128)(2,1)S(1)} all-to-all(bf16[16,2,1,8,768]{4,3,1,2,0:T(8,128)(2,1)S(1)} %copy.40), channel_id=1, replica_groups=mesh['ctx_0'=4,'ctx_1'=4,'ctx_2'=2,'tp'=8] {'ctx_0','ctx_1'}, dimensions={0} | all-to-all | bytes 786432 | tf_op jit(solution)/shard_map/all_to_all | solution.py:49
  125.9 1.8 fusion.29
  127.7 0.0 all-gather.2.cloned.1.call-update
  127.8 91.4 %all-gather.2.cloned.1.call-done = bf16[2048,768]{1,0:T(8,128)(2,1)} async-done(((bf16[256,768]{1,0:T(8,128)(2,1)}), bf16[2048,768]{1,0:T(8,128)(2,1)}) %all-gather.2.cloned.1.call-update) | async-done | bytes 3145744 | tf_op jit(solution)/shard_map/all_gather | solution.py:176
  219.2 0.0 copy-done
  219.2 5.0 %add_convert_fusion = bf16[768,512]{1,0:T(8,128)(2,1)} fusion(f32[768,4096]{1,0:T(8,128)} %get-tuple-element.13, s32[]{:T(128)S(6)} %select_n.86, bf16[2048,768]{1,0:T(8,128)(2,1)} %all-gather.2.cloned.1.call-done, bf16[2048,512]{1,0:T(8,128)(2,1)S(1)} %copy-done), kind=kOutput, calls=%fused_computation.23 | convolution fusion | flops 1611399168 | bytes 7602180 | tf_op jit(solution)/shard_map/dot_general | solution.py:175
  (4 shorter events, 0.1 us)
Async XLA Ops:
  6.5 212.6 %copy-start = (bf16[2048,512]{1,0:T(8,128)(2,1)S(1)}, bf16[2048,512]{1,0:T(8,128)(2,1)}, u32[]{:S(2)}) copy-start(bf16[2048,512]{1,0:T(8,128)(2,1)} %param.15) | copy-start | bytes 6291460
  15.4 8.7 %copy-start.4 = (f32[4096]{0:T(1024)S(1)}, f32[4096]{0:T(1024)}, u32[]{:S(2)}) copy-start(f32[4096]{0:T(1024)} %param.10) | copy-start | bytes 49156
  24.0 16.1 %copy-start.3 = (f32[3,3,256]{2,1,0:T(4,128)S(1)}, f32[3,3,256]{2,1,0:T(4,128)}, u32[]{:S(2)}) copy-start(f32[3,3,256]{2,1,0:T(4,128)} %param.12) | copy-start | bytes 27652
  35.2 7.5 %collective-permute-start = (bf16[3,256,2]{2,1,0:T(8,128)(2,1)S(1)}, bf16[3,256,2]{2,1,0:T(8,128)(2,1)S(1)}, u32[]{:S(2)}, u32[]{:S(2)}) collective-permute-start(bf16[3,256,2]{2,1,0:T(8,128)(2,1)S(1)} %slice.40), channel_id=1, source_target_pairs={{0,8},{8,16},{16,24},{24,32},{32,40},{40,48},{48,56},{56,64},{64,7... | collective-permute-start | bytes 9224 | tf_op jit(solution)/shard_map/ppermute | solution.py:15
  43.3 3.2 %copy-start.2 = (bf16[256,768]{1,0:T(8,128)(2,1)S(1)}, bf16[256,768]{1,0:T(8,128)(2,1)}, u32[]{:S(2)}) copy-start(bf16[256,768]{1,0:T(8,128)(2,1)} %param.13) | copy-start | bytes 1179652
  45.4 1.1 copy-start.1
  46.6 10.7 %copy-start.5 = (f32[256]{0:T(256)S(1)}, f32[256]{0:T(256)}, u32[]{:S(2)}) copy-start(f32[256]{0:T(256)} %param.14) | copy-start | bytes 3076
  47.5 31.8 %all-to-all-start = ((bf16[32,16,768]{2,1,0:T(8,128)(2,1)}), bf16[32,16,768]{2,1,0:T(8,128)(2,1)S(1)}, u32[]{:S(2)}, u32[]{:S(2)}) async-start(bf16[32,16,768]{2,1,0:T(8,128)(2,1)} %pad_maximum_fusion), calls=%async_computation | async-start | bytes 1572864 | tf_op jit(solution)/shard_map/all_to_all | solution.py:26
  57.0 162.2 %all-gather.2.cloned.1.call-start = ((), (), s32[]{:S(2)}) async-start(), calls=%async_computation.3 | async-start | bytes 3538944 | tf_op jit(solution)/shard_map/all_gather | solution.py:176
Sparse Core Ops, SparseCore 0:
  127.9 91.2 all-gather.1
where the time goes:
time: 232 us; the launch traced here: 231 us
  waiting for transfers between devices  115 us (50%)
  matrix products  47.6 us (21%)
  blocking collectives  19.9 us (9%)
  starting transfers between devices  14.6 us (6%)
  between operations  13.6 us (6%)
  local copies, waits for them, and re-layouts  12.4 us (5%)
  other arithmetic  7.86 us (3%)
    all_gather x1, waiting for transfers between devices, local(): lax.all_gather(gated, 'tp', axis=0, tiled=True)  91.4 us
    dot_general x18, matrix products, contract(): return jnp.einsum(form, left, right, preferred_element_type=jnp.float32)  22.6 us
    all_to_all x1, waiting for transfers between devices, sent_together(): lax.all_to_all(both, axis, split_axis=split_dim, concat_axis=concat_dim,...  21.2 us
    all_to_all x2, blocking collectives, turned_blocks(): out = lax.all_to_all(out, axes[k], k, k, tiled=True)  19.9 us
    dot_general x1, matrix products, local(): jnp.dot(normed, w_in.reshape(width, 3 * chan_part), preferred_element_typ...  11.1 us
    unnamed x13, local copies, waits for them, and re-layouts  9.78 us
    all_to_all x1, starting transfers between devices, sent_together(): lax.all_to_all(both, axis, split_axis=split_dim, concat_axis=concat_dim,...  9.47 us
    dot_general x1, matrix products, local(): embedded = jnp.dot(one_hot, embed_table, preferred_element_type=jnp.float32)  8.82 us
  transfers between devices with their start and end apart: 3, of which 3 were waited for; matrix products, arithmetic and copies ran while one was open for 0% of the time, Pallas kernels for 0%

commit v1 on v0

--- a/solution.py
+++ b/solution.py
@@ -7,6 +7,11 @@
 
 CTX = ("ctx_0", "ctx_1", "ctx_2")
 norm_eps = 1e-06
+
+
+def exchange_gather(block, axis, dim):
+    sent = jnp.stack([block] * lax.axis_size(axis))
+    return jnp.concatenate(lax.all_to_all(sent, axis, 0, 0), axis=dim)
 
 
 def shifted(block, axis, distance):
@@ -173,7 +178,7 @@
     gated = (query_side.astype(jnp.float32) * returned.astype(jnp.float32)).astype(jnp.bfloat16)
     width_part = w_out.shape[1]
     projected_out = jnp.dot(
-        lax.all_gather(gated, "tp", axis=0, tiled=True).T, w_out, preferred_element_type=jnp.float32
+        exchange_gather(gated, "tp", 0).T, w_out, preferred_element_type=jnp.float32
     )
     residual = lax.dynamic_slice_in_dim(embedded, lax.axis_index("tp") * width_part, width_part, 1)
     return (residual + projected_out).astype(jnp.bfloat16)

time: 232 us -> 210 us (0.905)
  waiting for transfers between devices: 115 us -> 94.3 us
  between operations: 13.6 us -> 0.23 us
  starting transfers between devices: 14.6 us -> 24 us
    all_gather x1 -> x0, waiting for transfers between devices: 91.4 us -> none  [local(): lax.all_gather(gated, 'tp', axis=0, tiled=True)]
    all_to_all x0 -> x1, waiting for transfers between devices: none -> 70.5 us  [exchange_gather(): return jnp.concatenate(lax.all_to_all(sent, axis, 0, 0), axis=dim)]
    all_to_all x0 -> x1, starting transfers between devices: none -> 9.45 us  [exchange_gather(): return jnp.concatenate(lax.all_to_all(sent, axis, 0, 0), axis=dim)]
where the time goes in v1:
time: 210 us; the launch traced here: 207 us
  waiting for transfers between devices  94.3 us (45%)
  matrix products  47.6 us (23%)
  starting transfers between devices  24 us (11%)
  blocking collectives  19.9 us (9%)
  local copies, waits for them, and re-layouts  14.3 us (7%)
  other arithmetic  7.11 us (3%)
    all_to_all x1, waiting for transfers between devices, exchange_gather(): return jnp.concatenate(lax.all_to_all(sent, axis, 0, 0), axis=dim)  70.5 us
    dot_general x18, matrix products, contract(): return jnp.einsum(form, left, right, preferred_element_type=jnp.float32)  22.6 us
    all_to_all x1, waiting for transfers between devices, sent_together(): lax.all_to_all(both, axis, split_axis=split_dim, concat_axis=concat_dim,...  21.2 us
    all_to_all x2, blocking collectives, turned_blocks(): out = lax.all_to_all(out, axes[k], k, k, tiled=True)  19.9 us
    dot_general x1, matrix products, local(): jnp.dot(normed, w_in.reshape(width, 3 * chan_part), preferred_element_typ...  11 us
    unnamed x13, local copies, waits for them, and re-layouts  9.8 us
    all_to_all x1, starting transfers between devices, sent_together(): lax.all_to_all(both, axis, split_axis=split_dim, concat_axis=concat_dim,...  9.66 us
    all_to_all x1, starting transfers between devices, exchange_gather(): return jnp.concatenate(lax.all_to_all(sent, axis, 0, 0), axis=dim)  9.45 us
  transfers between devices with their start and end apart: 3, of which 3 were waited for; matrix products, arithmetic and copies ran while one was open for 0% of the time, Pallas kernels for 0%

profile of v1, /device:TPU:1, one launch (start us, length us, event | category | flops | bytes accessed | tf_op | source)
XLA Modules:
  0.0 207.4 jit_solution(4210455993650197163)
XLA Ops:
  0.0 0.0 copy-start
  0.0 8.8 %multiply_reduce_fusion = (f32[768]{0:T(1024)S(1)}, f32[768,4096]{1,0:T(8,128)}) fusion(bf16[512,4096]{1,0:T(8,128)(2,1)} %param.9, s32[768]{0:T(1024)} %param.8), kind=kOutput, calls=%fused_computation.1 | convolution fusion | flops 3227909376 | bytes 16783360 | tf_op jit(solution)/shard_map/dot_general | solution.py:136
  8.8 0.0 copy-start.4
  8.8 8.7 %copy.32 = bf16[4096,3,256]{0,2,1:T(8,128)(2,1)} copy(bf16[4096,3,256]{2,0,1:T(8,128)(2,1)} %param.11) | data formatting | bytes 12582912 | tf_op args[3]
  17.5 0.0 copy-done.4
  17.5 0.0 copy-start.3
  17.5 11.0 %fusion.19 = bf16[768,768]{0,1:T(8,128)(2,1)S(1)} fusion(bf16[4096,768]{0,1:T(8,128)(2,1)} %bitcast.146, f32[768,4096]{1,0:T(8,128)} %get-tuple-element.13, f32[4096]{0:T(1024)S(1)} %copy-done.4, f32[768]{0:T(1024)S(1)} %add_rsqrt_fusion), kind=kOutput, calls=%fused_computation.36 | convolution fusion | flops 4841865216 | bytes 20073472 | tf_op jit(solution)/shard_map/dot_general | solution.py:141
  28.6 0.1 slice.40
  28.7 4.9 %collective-permute-start = (bf16[3,256,2]{2,1,0:T(8,128)(2,1)S(1)}, bf16[3,256,2]{2,1,0:T(8,128)(2,1)S(1)}, u32[]{:S(2)}, u32[]{:S(2)}) collective-permute-start(bf16[3,256,2]{2,1,0:T(8,128)(2,1)S(1)} %slice.40), channel_id=1, source_target_pairs={{0,8},{8,16},{16,24},{24,32},{32,40},{40,48},{48,56},{56,64},{64,7... | collective-permute-start | bytes 9224 | tf_op jit(solution)/shard_map/ppermute | solution.py:20
  33.6 0.0 copy-done.3
  33.7 2.6 %collective-permute-done = bf16[3,256,2]{2,1,0:T(8,128)(2,1)S(1)} collective-permute-done((bf16[3,256,2]{2,1,0:T(8,128)(2,1)S(1)}, bf16[3,256,2]{2,1,0:T(8,128)(2,1)S(1)}, u32[]{:S(2)}, u32[]{:S(2)}) %collective-permute-start) | collective-permute-done | bytes 3104 | tf_op jit(solution)/shard_map/ppermute | solution.py:20
  36.2 0.6 maximum_convert_fusion
  36.8 0.0 copy-start.2
  36.8 2.0 fusion.4
  38.9 0.0 copy-start.1
  38.9 1.1 copy-done.1
  39.9 0.1 fusion.37
  40.0 0.0 copy-done.2
  40.0 0.0 copy-start.5
  40.0 0.9 pad_maximum_fusion
  41.0 9.7 %all-to-all-start = ((bf16[32,16,768]{2,1,0:T(8,128)(2,1)}), bf16[32,16,768]{2,1,0:T(8,128)(2,1)S(1)}, u32[]{:S(2)}, u32[]{:S(2)}) async-start(bf16[32,16,768]{2,1,0:T(8,128)(2,1)} %pad_maximum_fusion), calls=%async_computation | async-start | bytes 1572864 | tf_op jit(solution)/shard_map/all_to_all | solution.py:31
  50.7 0.0 copy-done.5
  50.7 0.1 dynamic_slice.7
  50.7 0.8 fusion.85
  51.6 21.2 %all-to-all-done = bf16[32,16,768]{2,1,0:T(8,128)(2,1)S(1)} async-done(((bf16[32,16,768]{2,1,0:T(8,128)(2,1)}), bf16[32,16,768]{2,1,0:T(8,128)(2,1)S(1)}, u32[]{:S(2)}, u32[]{:S(2)}) %all-to-all-start) | async-done | bytes 786464 | tf_op jit(solution)/shard_map/all_to_all | solution.py:31
  72.8 0.1 copy.49
  72.8 0.1 fusion.205
  72.9 0.8 convolution_negate_fusion
  73.7 0.8 fusion.40
  74.4 0.8 convolution_negate_fusion.1
  75.2 0.8 fusion.43
  76.0 1.4 fusion.55
  77.4 1.4 fusion.59
  78.8 1.4 fusion.53
  80.2 1.4 fusion.49
  81.6 1.5 convolution_subtract_fusion.1
  83.0 1.4 convolution_add_fusion.2
  84.5 1.7 convolution_add_fusion.1
  86.1 1.8 multiply_add_fusion
  87.9 1.3 fusion.70
  89.2 1.3 fusion.72
  90.5 1.3 convolution_add_fusion
  91.9 1.3 convolution_subtract_fusion
  93.2 0.8 fusion.10
  94.0 1.7 fusion.26
  95.6 2.2 %reshape.131 = f32[1,8,32,768]{3,2,1,0:T(8,128)} reshape(f32[8,96,256]{2,1,0:T(8,128)} %fusion.26) | data formatting | bytes 1572864 | tf_op jit(solution)/shard_map/reshape | solution.py:128
  97.9 1.6 fusion.31
  99.5 3.8 %all_to_all.33 = bf16[16,2,1,8,768]{4,3,0,2,1:T(8,128)(2,1)S(1)} all-to-all(bf16[16,2,1,8,768]{4,3,0,2,1:T(8,128)(2,1)S(1)} %copy.39), channel_id=1, replica_groups=mesh['ctx_0'=4,'ctx_1'=4,'ctx_2'=2,'tp'=8] {'ctx_2'}, dimensions={1} | all-to-all | bytes 786432 | tf_op jit(solution)/shard_map/all_to_all | solution.py:54
  103.3 16.1 %all_to_all.34 = bf16[16,2,1,8,768]{4,3,1,2,0:T(8,128)(2,1)S(1)} all-to-all(bf16[16,2,1,8,768]{4,3,1,2,0:T(8,128)(2,1)S(1)} %copy.40), channel_id=1, replica_groups=mesh['ctx_0'=4,'ctx_1'=4,'ctx_2'=2,'tp'=8] {'ctx_0','ctx_1'}, dimensions={0} | all-to-all | bytes 786432 | tf_op jit(solution)/shard_map/all_to_all | solution.py:54
  119.4 1.1 fusion.38
  120.5 1.8 stack.5
  122.3 9.5 %all-to-all-start.3 = ((bf16[8,256,768]{2,1,0:T(8,128)(2,1)}), bf16[8,256,768]{2,1,0:T(8,128)(2,1)}, u32[]{:S(2)}, u32[]{:S(2)}) async-start(bf16[8,256,768]{2,1,0:T(8,128)(2,1)} %stack.5), calls=%async_computation.3 | async-start | bytes 6291456 | tf_op jit(solution)/shard_map/all_to_all | solution.py:14
  131.8 70.5 %all-to-all-done.3 = bf16[8,256,768]{2,1,0:T(8,128)(2,1)} async-done(((bf16[8,256,768]{2,1,0:T(8,128)(2,1)}), bf16[8,256,768]{2,1,0:T(8,128)(2,1)}, u32[]{:S(2)}, u32[]{:S(2)}) %all-to-all-start.3) | async-done | bytes 3145760 | tf_op jit(solution)/shard_map/all_to_all | solution.py:14
  202.3 0.0 copy-done
  202.3 5.0 %add_convert_fusion = bf16[768,512]{1,0:T(8,128)(2,1)} fusion(f32[768,4096]{1,0:T(8,128)} %get-tuple-element.13, s32[]{:T(128)S(6)} %select_n.86, bf16[2048,768]{1,0:T(8,128)(2,1)} %bitcast.28, bf16[2048,512]{1,0:T(8,128)(2,1)S(1)} %copy-done), kind=kOutput, calls=%fused_computation.23 | convolution fusion | flops 1611399168 | bytes 7602180 | tf_op jit(solution)/shard_map/dot_general | solution.py:180
  (4 shorter events, 0.1 us)
Async XLA Ops:
  0.0 202.3 %copy-start = (bf16[2048,512]{1,0:T(8,128)(2,1)S(1)}, bf16[2048,512]{1,0:T(8,128)(2,1)}, u32[]{:S(2)}) copy-start(bf16[2048,512]{1,0:T(8,128)(2,1)} %param.15) | copy-start | bytes 6291460
  8.8 8.7 %copy-start.4 = (f32[4096]{0:T(1024)S(1)}, f32[4096]{0:T(1024)}, u32[]{:S(2)}) copy-start(f32[4096]{0:T(1024)} %param.10) | copy-start | bytes 49156
  17.5 16.1 %copy-start.3 = (f32[3,3,256]{2,1,0:T(4,128)S(1)}, f32[3,3,256]{2,1,0:T(4,128)}, u32[]{:S(2)}) copy-start(f32[3,3,256]{2,1,0:T(4,128)} %param.12) | copy-start | bytes 27652
  28.7 7.5 %collective-permute-start = (bf16[3,256,2]{2,1,0:T(8,128)(2,1)S(1)}, bf16[3,256,2]{2,1,0:T(8,128)(2,1)S(1)}, u32[]{:S(2)}, u32[]{:S(2)}) collective-permute-start(bf16[3,256,2]{2,1,0:T(8,128)(2,1)S(1)} %slice.40), channel_id=1, source_target_pairs={{0,8},{8,16},{16,24},{24,32},{32,40},{40,48},{48,56},{56,64},{64,7... | collective-permute-start | bytes 9224 | tf_op jit(solution)/shard_map/ppermute | solution.py:20
  36.8 3.2 %copy-start.2 = (bf16[256,768]{1,0:T(8,128)(2,1)S(1)}, bf16[256,768]{1,0:T(8,128)(2,1)}, u32[]{:S(2)}) copy-start(bf16[256,768]{1,0:T(8,128)(2,1)} %param.13) | copy-start | bytes 1179652
  38.9 1.1 copy-start.1
  40.0 10.6 %copy-start.5 = (f32[256]{0:T(256)S(1)}, f32[256]{0:T(256)}, u32[]{:S(2)}) copy-start(f32[256]{0:T(256)} %param.14) | copy-start | bytes 3076
  41.0 31.8 %all-to-all-start = ((bf16[32,16,768]{2,1,0:T(8,128)(2,1)}), bf16[32,16,768]{2,1,0:T(8,128)(2,1)S(1)}, u32[]{:S(2)}, u32[]{:S(2)}) async-start(bf16[32,16,768]{2,1,0:T(8,128)(2,1)} %pad_maximum_fusion), calls=%async_computation | async-start | bytes 1572864 | tf_op jit(solution)/shard_map/all_to_all | solution.py:31
  122.3 80.0 %all-to-all-start.3 = ((bf16[8,256,768]{2,1,0:T(8,128)(2,1)}), bf16[8,256,768]{2,1,0:T(8,128)(2,1)}, u32[]{:S(2)}, u32[]{:S(2)}) async-start(bf16[8,256,768]{2,1,0:T(8,128)(2,1)} %stack.5), calls=%async_computation.3 | async-start | bytes 6291456 | tf_op jit(solution)/shard_map/all_to_all | solution.py:14
